TPU v7x, 512 devices: a whole 4x4x16 slice. The times are simulated.
512 devices in a mesh: fsdp: 128 (over x, z, core), grp: 4 (over y).
Axes of the slice: x: 4, y: 4, z: 16, core: 2. Of those that a mesh axis runs over, the one named last changes fastest.
Arguments:
- grad: bfloat16 [28672, 8192], P('fsdp', 'grp'), may hold values from -6 to 6
- projector_t: bfloat16 [1024, 8192], P('fsdp', 'grp'), may hold values from -0.0625 to 0.0625
- first_moment: float32 [28672, 1024], P('fsdp', 'grp'), may hold values from -3 to 3
- second_moment: float32 [28672, 1024], P('fsdp', 'grp'), may hold values from 0.0001 to 0.01
Outputs:
- update: float32 [28672, 8192], P('fsdp', 'grp')
- first_new: float32 [28672, 1024], P('fsdp', 'grp')
- second_new: float32 [28672, 1024], P('fsdp', 'grp')
All inputs are finite; a program needn't handle non-finite values.
Results may differ from a plain program's by a relative error of at most 0.0029.
Values may be sent and summed in bfloat16 or wider, within the bound.
No kernel may reach another device: no remote copies, remote signals or barrier semaphores. Data moves between devices by JAX's collectives and lax.ppermute only.
A program may use at most 64 MiB of HBM per device.

v0:
```python
import jax
import jax.numpy as jnp
from jax import lax
from jax.experimental import pallas as pl
from jax.experimental.pallas import tpu as pltpu
from jax.sharding import Mesh
from jax.sharding import PartitionSpec as P


STEP = 10
FSDP = ("x", "z", "c")
VMEM = pl.BlockSpec(memory_space=pltpu.VMEM)
ROTATED = [[4 * x + (x + d) % 4 for d in range(4)] for x in range(4)]


def exchange(parts):
    return lax.all_to_all(parts, ("x", "y"), 0, 0, axis_index_groups=ROTATED, tiled=True)


def encode(part):
    scaled = part * 2.0**22
    square = scaled * scaled
    return jnp.where(part < 0.0, -square * square, square * square).astype(jnp.bfloat16)


def decode(sent):
    fourth = sent.astype(jnp.float32)
    size = jnp.sqrt(jnp.sqrt(jnp.abs(fourth))) * 2.0**-22
    return jnp.where(fourth < 0.0, -size, size)


def project(grad, own, other):
    rows = jnp.concatenate([own[...], other[...]], axis=0)
    return lax.dot_general(
        grad[...], rows, (((1,), (1,)), ((), ())), preferred_element_type=jnp.float32
    )


def first_block(grad, own, other, part):
    part[...] = encode(project(grad, own, other))


def middle_blocks(grad, own_1, other_1, own_3, other_3, part_1, part_3):
    part_1[...] = encode(project(grad, own_1, other_1))
    part_3[...] = encode(project(grad, own_3, other_3))


def last_block(grad, own, other, part_0, part_1, part_3, out):
    out[0] = part_0[...]
    out[1] = part_1[...]
    out[3] = part_3[...]
    out[2] = encode(project(grad, own, other))


def moments(received, first, second, first_out, second_out, copies):
    at = lax.broadcasted_iota(jnp.int32, (256, 256), 0)
    rank = lax.broadcasted_iota(jnp.int32, (256, 256), 1)
    half = jnp.bitwise_xor(lax.shift_right_logical(at, 7), lax.axis_index("c"))
    spot = (lax.shift_right_logical(at, 3) & 15) * 16 + half * 8 + (at & 7)
    place = (rank == spot).astype(jnp.bfloat16)
    left = decode(received[0])
    for k in (1, 2, 3):
        left += decode(received[k])
    projected = jnp.zeros(first.shape, jnp.float32)
    for _ in range(3):
        piece = left.astype(jnp.bfloat16)
        projected += jnp.dot(piece, place, preferred_element_type=jnp.float32)
        left = left - piece.astype(jnp.float32)
    first_new = 0.9 * first[...] + 0.1 * projected
    second_new = 0.999 * second[...] + 0.001 * projected * projected
    first_out[...] = first_new
    second_out[...] = second_new
    correct_one = 1.0 - 0.9**STEP
    correct_two = 1.0 - 0.999**STEP
    normalized = (first_new / correct_one / (jnp.sqrt(second_new / correct_two) + 1e-08)).astype(
        jnp.bfloat16
    )
    turned = lax.dot_general(
        normalized, place, (((1,), (1,)), ((), ())), preferred_element_type=jnp.float32
    ).astype(jnp.bfloat16)
    for k in range(4):
        copies[k] = turned


def back(steps, first, second, *refs):
    pieces, (out, first_out, second_out, held, sems) = refs[:8], refs[8:]
    width = 512
    sent = [
        pltpu.make_async_copy(first, first_out, sems.at[4]),
        pltpu.make_async_copy(second, second_out, sems.at[5]),
    ]
    for copy in sent:
        copy.start()
    for k in range(4):
        columns = pl.ds(k * width, width)
        total = jnp.zeros((steps.shape[1], width), jnp.float32)
        for d in range(4):
            rows = jnp.concatenate(
                [pieces[2 * d][:, columns], pieces[2 * d + 1][:, columns]], axis=0
            )
            total += jnp.dot(steps[d], rows, preferred_element_type=jnp.float32)
        held[:, columns] = total
        copy = pltpu.make_async_copy(held.at[:, columns], out.at[:, columns], sems.at[k])
        copy.start()
        sent.append(copy)
    for copy in sent:
        copy.wait()


def limit(mib):
    return pltpu.CompilerParams(vmem_limit_bytes=mib * 2**20)


def call(kernel, out_shape, *operands):
    many = isinstance(out_shape, tuple)
    return pl.pallas_call(
        kernel,
        out_shape=out_shape,
        in_specs=[VMEM] * len(operands),
        out_specs=(VMEM,) * len(out_shape) if many else VMEM,
        compiler_params=limit(8),
    )(*operands)


def step(grad, projector_t, first_moment, second_moment):
    own = lax.all_gather(projector_t, "z", axis=0, tiled=True)

    def from_x(d):
        return lax.ppermute(own, "x", [(x, (x - d) % 4) for x in range(4)])

    def from_core(d):
        return lax.ppermute(blocks[d], "c", [(0, 1), (1, 0)])

    blocks = {0: own}
    for d in (1, 3, 2):
        blocks[d] = from_x(d)
    others = {d: from_core(d) for d in (0, 1, 3, 2)}
    columns, ranks = first_moment.shape
    one = jax.ShapeDtypeStruct((columns, ranks), jnp.bfloat16)
    four = jax.ShapeDtypeStruct((4, columns, ranks), jnp.bfloat16)
    held = jax.ShapeDtypeStruct((columns, ranks), jnp.float32)
    part_0 = call(first_block, one, grad, blocks[0], others[0])
    part_1, part_3 = call(
        middle_blocks, (one, one), grad, blocks[1], others[1], blocks[3], others[3]
    )
    parts = call(last_block, four, grad, blocks[2], others[2], part_0, part_1, part_3)
    received = exchange(parts)
    first_new, second_new, copies = call(
        moments, (held, held, four), received, first_moment, second_moment
    )
    steps = exchange(copies)
    width = projector_t.shape[1]
    HBM = pl.BlockSpec(memory_space=pl.ANY)
    return pl.pallas_call(
        back,
        out_shape=(jax.ShapeDtypeStruct((columns, width), jnp.float32), held, held),
        in_specs=[VMEM] * 11,
        out_specs=(HBM,) * 3,
        scratch_shapes=[pltpu.VMEM((columns, width), jnp.float32), pltpu.SemaphoreType.DMA((6,))],
        compiler_params=limit(8),
        name="back",
    )(steps, first_new, second_new, *[half[d] for d in range(4) for half in (blocks, others)])


def solution(mesh):
    finer = Mesh(mesh.devices.reshape(4, 16, 2, 4), ("x", "z", "c", "y"))
    spec = P(FSDP, "y")
    return jax.shard_map(
        step, mesh=finer, in_specs=(spec,) * 4, out_specs=(spec,) * 3, check_vma=False
    )
```

profile of v0, /device:TPU:6, one launch (start us, length us, event | category | flops | bytes accessed | tf_op | source)
XLA Modules:
  0.0 95.6 jit_solution(12356669406466364978)
XLA Ops:
  0.6 38.8 %all_gather.3.own.refs_0_ = bf16[128,2048]{1,0:T(8,128)(2,1)S(1)} all-gather(bf16[8,2048]{1,0:T(8,128)(2,1)} %param.5), channel_id=1, replica_groups=mesh['x'=4,'z'=16,'c'=2,'y'=4] {'z'}, dimensions={0}, use_global_device_ids=true | all-gather | bytes 557056 | tf_op jit(solution)/shard_map/all_gather | solution.py:126
  39.4 2.4 %collective-permute-start.5 = (bf16[128,2048]{1,0:T(8,128)(2,1)S(1)}, bf16[128,2048]{1,0:T(8,128)(2,1)S(1)}, u32[]{:S(2)}, u32[]{:S(2)}) collective-permute-start(bf16[128,2048]{1,0:T(8,128)(2,1)S(1)} %all_gather.3.own.refs_0_), channel_id=1, source_target_pairs={{0,128},{128,256},{256,384},{384,0},{1,129},{129,257},{257,385},{3... | collective-permute-start | bytes 1572872 | tf_op jit(solution)/shard_map/ppermute | solution.py:129
  41.8 3.5 %collective-permute-start.3 = (bf16[128,2048]{1,0:T(8,128)(2,1)S(1)}, bf16[128,2048]{1,0:T(8,128)(2,1)S(1)}, u32[]{:S(2)}, u32[]{:S(2)}) collective-permute-start(bf16[128,2048]{1,0:T(8,128)(2,1)S(1)} %all_gather.3.own.refs_0_), channel_id=1, source_target_pairs={{0,384},{128,0},{256,128},{384,256},{1,385},{129,1},{257,129},{385... | collective-permute-start | bytes 1572872 | tf_op jit(solution)/shard_map/ppermute | solution.py:129
  45.3 3.3 %collective-permute-start = (bf16[128,2048]{1,0:T(8,128)(2,1)S(1)}, bf16[128,2048]{1,0:T(8,128)(2,1)S(1)}, u32[]{:S(2)}, u32[]{:S(2)}) collective-permute-start(bf16[128,2048]{1,0:T(8,128)(2,1)S(1)} %all_gather.3.own.refs_0_), channel_id=1, source_target_pairs={{0,256},{128,384},{256,0},{384,128},{1,257},{129,385},{257,1},{385... | collective-permute-start | bytes 1572872 | tf_op jit(solution)/shard_map/ppermute | solution.py:129
  48.6 1.9 %collective-permute-start.2 = (bf16[128,2048]{1,0:T(8,128)(2,1)S(1)}, bf16[128,2048]{1,0:T(8,128)(2,1)S(1)}, u32[]{:S(2)}, u32[]{:S(2)}) collective-permute-start(bf16[128,2048]{1,0:T(8,128)(2,1)S(1)} %all_gather.3.own.refs_0_), channel_id=1, source_target_pairs={{0,4},{4,0},{1,5},{5,1},{2,6},{6,2},{3,7},{7,3},{8,12},{12,8},{9,1... | collective-permute-start | bytes 1572872 | tf_op jit(solution)/shard_map/ppermute | solution.py:132
  50.5 2.7 %collective-permute-done.5.own_3.refs_6_ = bf16[128,2048]{1,0:T(8,128)(2,1)S(1)} collective-permute-done((bf16[128,2048]{1,0:T(8,128)(2,1)S(1)}, bf16[128,2048]{1,0:T(8,128)(2,1)S(1)}, u32[]{:S(2)}, u32[]{:S(2)}) %collective-permute-start.5) | collective-permute-done | bytes 524320 | tf_op jit(solution)/shard_map/ppermute | solution.py:129
  53.2 1.9 %collective-permute-start.6 = (bf16[128,2048]{1,0:T(8,128)(2,1)S(1)}, bf16[128,2048]{1,0:T(8,128)(2,1)S(1)}, u32[]{:S(2)}, u32[]{:S(2)}) collective-permute-start(bf16[128,2048]{1,0:T(8,128)(2,1)S(1)} %collective-permute-done.5.own_3.refs_6_), channel_id=1, source_target_pairs={{0,4},{4,0},{1,5},{5,1},{2,6},{6,2},{3,7},{7,3},{8,12},{12,8},{9,1... | collective-permute-start | bytes 1572872 | tf_op jit(solution)/shard_map/ppermute | solution.py:132
  55.1 6.8 %collective-permute-done.3.own_1.refs_2_ = bf16[128,2048]{1,0:T(8,128)(2,1)S(1)} collective-permute-done((bf16[128,2048]{1,0:T(8,128)(2,1)S(1)}, bf16[128,2048]{1,0:T(8,128)(2,1)S(1)}, u32[]{:S(2)}, u32[]{:S(2)}) %collective-permute-start.3) | collective-permute-done | bytes 524320 | tf_op jit(solution)/shard_map/ppermute | solution.py:129
  62.0 1.9 %collective-permute-start.4 = (bf16[128,2048]{1,0:T(8,128)(2,1)S(1)}, bf16[128,2048]{1,0:T(8,128)(2,1)S(1)}, u32[]{:S(2)}, u32[]{:S(2)}) collective-permute-start(bf16[128,2048]{1,0:T(8,128)(2,1)S(1)} %collective-permute-done.3.own_1.refs_2_), channel_id=1, source_target_pairs={{0,4},{4,0},{1,5},{5,1},{2,6},{6,2},{3,7},{7,3},{8,12},{12,8},{9,1... | collective-permute-start | bytes 1572872 | tf_op jit(solution)/shard_map/ppermute | solution.py:132
  63.9 0.0 collective-permute-done.own.refs_4_
  63.9 2.4 %collective-permute-start.1 = (bf16[128,2048]{1,0:T(8,128)(2,1)S(1)}, bf16[128,2048]{1,0:T(8,128)(2,1)S(1)}, u32[]{:S(2)}, u32[]{:S(2)}) collective-permute-start(bf16[128,2048]{1,0:T(8,128)(2,1)S(1)} %collective-permute-done.own.refs_4_), channel_id=1, source_target_pairs={{0,4},{4,0},{1,5},{5,1},{2,6},{6,2},{3,7},{7,3},{8,12},{12,8},{9,1... | collective-permute-start | bytes 1572872 | tf_op jit(solution)/shard_map/ppermute | solution.py:132
  66.3 0.0 collective-permute-done.2.other.refs_1_
  66.3 0.0 copy-start
  66.3 1.2 %copy-done = bf16[224,2048]{1,0:T(8,128)(2,1)S(1)} copy-done((bf16[224,2048]{1,0:T(8,128)(2,1)S(1)}, bf16[224,2048]{1,0:T(8,128)(2,1)}, u32[]{:S(2)}) %copy-start) | copy-done | bytes 917528
  67.5 0.5 shard_map.67.part_0
  68.0 0.0 collective-permute-done.4.other_1.refs_3_
  68.0 0.8 shard_map.68
  68.9 0.0 copy-start.1
  68.9 0.0 copy-start.2
  68.9 0.5 shard_map.69
  69.4 12.6 %all_to_all.10.received = bf16[4,224,256]{2,1,0:T(8,128)(2,1)S(1)} all-to-all(bf16[4,224,256]{2,1,0:T(8,128)(2,1)S(1)} %shard_map.69), channel_id=1, replica_groups={{0,1,2,3},{129,130,131,128},{258,259,256,257},{387,384,385,386},{4,5,6,..., dimensions={0} | all-to-all | bytes 917504 | tf_op jit(solution)/shard_map/all_to_all | solution.py:17
  82.0 1.2 %shard_map.70 = (f32[224,256]{1,0:T(8,128)S(1)}, f32[224,256]{1,0:T(8,128)S(1)}, bf16[4,224,256]{2,1,0:T(8,128)(2,1)S(1)}) custom-call(bf16[4,224,256]{2,1,0:T(8,128)(2,1)S(1)} %all_to_all.10.received, f32[224,256]{1,0:T(8,128)S(1)} %copy-done.1, f32[224,256]{1,0:T(8,128)S(1)} %copy-done.2), custom_call_target="tpu_custom_call" | custom-call | tf_op jit(solution)/shard_map/pallas_call | solution.py:116
  83.1 10.6 %all_to_all.11.steps = bf16[4,224,256]{2,1,0:T(8,128)(2,1)S(1)} all-to-all(bf16[4,224,256]{2,1,0:T(8,128)(2,1)S(1)} %get-tuple-element.10), channel_id=1, replica_groups={{0,1,2,3},{129,130,131,128},{258,259,256,257},{387,384,385,386},{4,5,6,..., dimensions={0} | all-to-all | bytes 917504 | tf_op jit(solution)/shard_map/all_to_all | solution.py:17
  93.7 1.9 %back.1 = (f32[224,2048]{1,0:T(8,128)}, f32[224,256]{1,0:T(8,128)}, f32[224,256]{1,0:T(8,128)}) custom-call(bf16[4,224,256]{2,1,0:T(8,128)(2,1)S(1)} %all_to_all.11.steps, f32[224,256]{1,0:T(8,128)S(1)} %get-tuple-element.11.first, f32[224,256]{1,0:T(8,128)S(1)} %get-tuple-element.12.second, bf16[128,2048]{1,0:T(8,128)(2,1)S(1)} %all_gather.3.own.refs_0_, ...), custom_call_target="tpu_custom_call" | custom-call | tf_op jit(solution)/shard_map/back/pallas_call | solution.py:154
  (4 shorter events, 0.0 us)
Async XLA Ops:
  39.4 13.8 %collective-permute-start.5 = (bf16[128,2048]{1,0:T(8,128)(2,1)S(1)}, bf16[128,2048]{1,0:T(8,128)(2,1)S(1)}, u32[]{:S(2)}, u32[]{:S(2)}) collective-permute-start(bf16[128,2048]{1,0:T(8,128)(2,1)S(1)} %all_gather.3.own.refs_0_), channel_id=1, source_target_pairs={{0,128},{128,256},{256,384},{384,0},{1,129},{129,257},{257,385},{3... | collective-permute-start | bytes 1572872 | tf_op jit(solution)/shard_map/ppermute | solution.py:129
  41.8 20.2 %collective-permute-start.3 = (bf16[128,2048]{1,0:T(8,128)(2,1)S(1)}, bf16[128,2048]{1,0:T(8,128)(2,1)S(1)}, u32[]{:S(2)}, u32[]{:S(2)}) collective-permute-start(bf16[128,2048]{1,0:T(8,128)(2,1)S(1)} %all_gather.3.own.refs_0_), channel_id=1, source_target_pairs={{0,384},{128,0},{256,128},{384,256},{1,385},{129,1},{257,129},{385... | collective-permute-start | bytes 1572872 | tf_op jit(solution)/shard_map/ppermute | solution.py:129
  45.3 18.6 %collective-permute-start = (bf16[128,2048]{1,0:T(8,128)(2,1)S(1)}, bf16[128,2048]{1,0:T(8,128)(2,1)S(1)}, u32[]{:S(2)}, u32[]{:S(2)}) collective-permute-start(bf16[128,2048]{1,0:T(8,128)(2,1)S(1)} %all_gather.3.own.refs_0_), channel_id=1, source_target_pairs={{0,256},{128,384},{256,0},{384,128},{1,257},{129,385},{257,1},{385... | collective-permute-start | bytes 1572872 | tf_op jit(solution)/shard_map/ppermute | solution.py:129
  48.6 17.7 %collective-permute-start.2 = (bf16[128,2048]{1,0:T(8,128)(2,1)S(1)}, bf16[128,2048]{1,0:T(8,128)(2,1)S(1)}, u32[]{:S(2)}, u32[]{:S(2)}) collective-permute-start(bf16[128,2048]{1,0:T(8,128)(2,1)S(1)} %all_gather.3.own.refs_0_), channel_id=1, source_target_pairs={{0,4},{4,0},{1,5},{5,1},{2,6},{6,2},{3,7},{7,3},{8,12},{12,8},{9,1... | collective-permute-start | bytes 1572872 | tf_op jit(solution)/shard_map/ppermute | solution.py:132
  53.2 14.8 %collective-permute-start.6 = (bf16[128,2048]{1,0:T(8,128)(2,1)S(1)}, bf16[128,2048]{1,0:T(8,128)(2,1)S(1)}, u32[]{:S(2)}, u32[]{:S(2)}) collective-permute-start(bf16[128,2048]{1,0:T(8,128)(2,1)S(1)} %collective-permute-done.5.own_3.refs_6_), channel_id=1, source_target_pairs={{0,4},{4,0},{1,5},{5,1},{2,6},{6,2},{3,7},{7,3},{8,12},{12,8},{9,1... | collective-permute-start | bytes 1572872 | tf_op jit(solution)/shard_map/ppermute | solution.py:132
  62.0 6.0 %collective-permute-start.4 = (bf16[128,2048]{1,0:T(8,128)(2,1)S(1)}, bf16[128,2048]{1,0:T(8,128)(2,1)S(1)}, u32[]{:S(2)}, u32[]{:S(2)}) collective-permute-start(bf16[128,2048]{1,0:T(8,128)(2,1)S(1)} %collective-permute-done.3.own_1.refs_2_), channel_id=1, source_target_pairs={{0,4},{4,0},{1,5},{5,1},{2,6},{6,2},{3,7},{7,3},{8,12},{12,8},{9,1... | collective-permute-start | bytes 1572872 | tf_op jit(solution)/shard_map/ppermute | solution.py:132
  63.9 5.0 %collective-permute-start.1 = (bf16[128,2048]{1,0:T(8,128)(2,1)S(1)}, bf16[128,2048]{1,0:T(8,128)(2,1)S(1)}, u32[]{:S(2)}, u32[]{:S(2)}) collective-permute-start(bf16[128,2048]{1,0:T(8,128)(2,1)S(1)} %collective-permute-done.own.refs_4_), channel_id=1, source_target_pairs={{0,4},{4,0},{1,5},{5,1},{2,6},{6,2},{3,7},{7,3},{8,12},{12,8},{9,1... | collective-permute-start | bytes 1572872 | tf_op jit(solution)/shard_map/ppermute | solution.py:132
  66.3 1.2 %copy-start = (bf16[224,2048]{1,0:T(8,128)(2,1)S(1)}, bf16[224,2048]{1,0:T(8,128)(2,1)}, u32[]{:S(2)}) copy-start(bf16[224,2048]{1,0:T(8,128)(2,1)} %grad.5) | copy-start | bytes 2752516
  68.9 13.1 %copy-start.1 = (f32[224,256]{1,0:T(8,128)S(1)}, f32[224,256]{1,0:T(8,128)}, u32[]{:S(2)}) copy-start(f32[224,256]{1,0:T(8,128)} %first.1) | copy-start | bytes 688132
  68.9 13.1 %copy-start.2 = (f32[224,256]{1,0:T(8,128)S(1)}, f32[224,256]{1,0:T(8,128)}, u32[]{:S(2)}) copy-start(f32[224,256]{1,0:T(8,128)} %second.1) | copy-start | bytes 688132
where the time goes:
time: 96 us; the launch traced here: 95.6 us
  blocking collectives  61.9 us (64%)
  starting transfers between devices  17.3 us (18%)
  waiting for transfers between devices  9.54 us (10%)
  Pallas kernels  4.92 us (5%)
  local copies, waits for them, and re-layouts  1.19 us (1%)
    all_gather x1, blocking collectives, step(): own = lax.all_gather(projector_t, 'z', axis=0, tiled=True)  38.8 us
    all_to_all x2, blocking collectives, exchange(): lax.all_to_all(parts, ('x', 'y'), 0, 0, axis_index_groups=ROTATED, tiled=...  23.1 us
    ppermute x3, waiting for transfers between devices, from_x(): return lax.ppermute(own, 'x', [(x, (x - d) % 4) for x in range(4)])  9.53 us
    ppermute x3, starting transfers between devices, from_x(): return lax.ppermute(own, 'x', [(x, (x - d) % 4) for x in range(4)])  9.15 us
    ppermute x4, starting transfers between devices, from_core(): return lax.ppermute(blocks[d], 'c', [(0, 1), (1, 0)])  8.14 us
    pallas_call x4, Pallas kernels, call(): pl.pallas_call(kernel, out_shape=out_shape, in_specs=[VMEM] * len(operand...  2.98 us
    pallas_call x1, Pallas kernels, step(): pl.pallas_call(back, out_shape=(jax.ShapeDtypeStruct((columns, width), jn...  1.94 us
  transfers between devices with their start and end apart: 7, of which 2 were waited for; matrix products, arithmetic and copies ran while one was open for 0% of the time, Pallas kernels for 1%

commit v1 on v0

--- a/solution.py
+++ b/solution.py
@@ -11,10 +11,15 @@
 FSDP = ("x", "z", "c")
 VMEM = pl.BlockSpec(memory_space=pltpu.VMEM)
 ROTATED = [[4 * x + (x + d) % 4 for d in range(4)] for x in range(4)]
+BOTH = [[(2 * x + c) * 4 + (x + d) % 4 for c in range(2) for d in range(4)] for x in range(4)]
 
 
 def exchange(parts):
     return lax.all_to_all(parts, ("x", "y"), 0, 0, axis_index_groups=ROTATED, tiled=True)
+
+
+def exchange_both(parts):
+    return lax.all_to_all(parts, ("x", "c", "y"), 0, 0, axis_index_groups=BOTH, tiled=True)
 
 
 def encode(part):
@@ -29,38 +34,48 @@
     return jnp.where(fourth < 0.0, -size, size)
 
 
-def project(grad, own, other):
-    rows = jnp.concatenate([own[...], other[...]], axis=0)
-    return lax.dot_general(
-        grad[...], rows, (((1,), (1,)), ((), ())), preferred_element_type=jnp.float32
-    )
-
-
-def first_block(grad, own, other, part):
-    part[...] = encode(project(grad, own, other))
-
-
-def middle_blocks(grad, own_1, other_1, own_3, other_3, part_1, part_3):
-    part_1[...] = encode(project(grad, own_1, other_1))
-    part_3[...] = encode(project(grad, own_3, other_3))
-
-
-def last_block(grad, own, other, part_0, part_1, part_3, out):
-    out[0] = part_0[...]
-    out[1] = part_1[...]
-    out[3] = part_3[...]
-    out[2] = encode(project(grad, own, other))
+def project(own, swapped, rows, parts):
+    for k, grad in enumerate((own, swapped)):
+        parts[k] = encode(
+            lax.dot_general(
+                grad[...], rows, (((1,), (1,)), ((), ())), preferred_element_type=jnp.float32
+            )
+        )
+
+
+def first_block(own, swapped, rows, parts):
+    project(own, swapped, rows[...], parts)
+
+
+def middle_block(own, swapped, rows, parts):
+    project(own, swapped, rows[...], parts)
+
+
+def last_blocks(own, swapped, rows_1, rows_2, parts_0, parts_3, out, pair, held):
+    core = lax.axis_index("c")
+    rows = jnp.concatenate([rows_1[...], rows_2[...]], axis=0)
+    pair[...] = rows
+    project(own, swapped, rows, held)
+    for k in range(2):
+        slot = 4 * jnp.bitwise_xor(core, k)
+        out[slot] = parts_0[k]
+        out[slot + 1] = held[k, :, :128]
+        out[slot + 2] = held[k, :, 128:]
+        out[slot + 3] = parts_3[k]
 
 
 def moments(received, first, second, first_out, second_out, copies):
     at = lax.broadcasted_iota(jnp.int32, (256, 256), 0)
     rank = lax.broadcasted_iota(jnp.int32, (256, 256), 1)
-    half = jnp.bitwise_xor(lax.shift_right_logical(at, 7), lax.axis_index("c"))
+    core = lax.axis_index("c")
+    half = jnp.bitwise_xor(lax.shift_right_logical(at, 7), core)
     spot = (lax.shift_right_logical(at, 3) & 15) * 16 + half * 8 + (at & 7)
     place = (rank == spot).astype(jnp.bfloat16)
-    left = decode(received[0])
-    for k in (1, 2, 3):
-        left += decode(received[k])
+    halves = []
+    for k in range(2):
+        slot = 4 * jnp.bitwise_xor(core, k)
+        halves.append(sum(decode(received[slot + d]) for d in range(4)))
+    left = jnp.concatenate(halves, axis=1)
     projected = jnp.zeros(first.shape, jnp.float32)
     for _ in range(3):
         piece = left.astype(jnp.bfloat16)
@@ -83,7 +98,9 @@
 
 
 def back(steps, first, second, *refs):
-    pieces, (out, first_out, second_out, held, sems) = refs[:8], refs[8:]
+    (own_0, other_0, pair, other_pair, own_3, other_3), refs = refs[:6], refs[6:]
+    out, first_out, second_out, held, sems = refs
+    low, high = pl.ds(0, 128), pl.ds(128, 128)
     width = 512
     sent = [
         pltpu.make_async_copy(first, first_out, sems.at[4]),
@@ -94,10 +111,15 @@
     for k in range(4):
         columns = pl.ds(k * width, width)
         total = jnp.zeros((steps.shape[1], width), jnp.float32)
-        for d in range(4):
-            rows = jnp.concatenate(
-                [pieces[2 * d][:, columns], pieces[2 * d + 1][:, columns]], axis=0
+        for d, (one, two, where) in enumerate(
+            (
+                (own_0, other_0, low),
+                (pair, other_pair, low),
+                (pair, other_pair, high),
+                (own_3, other_3, low),
             )
+        ):
+            rows = jnp.concatenate([one[where, columns], two[where, columns]], axis=0)
             total += jnp.dot(steps[d], rows, preferred_element_type=jnp.float32)
         held[:, columns] = total
         copy = pltpu.make_async_copy(held.at[:, columns], out.at[:, columns], sems.at[k])
@@ -128,23 +150,33 @@
     def from_x(d):
         return lax.ppermute(own, "x", [(x, (x - d) % 4) for x in range(4)])
 
-    def from_core(d):
-        return lax.ppermute(blocks[d], "c", [(0, 1), (1, 0)])
+    def from_core(block):
+        return lax.ppermute(block, "c", [(0, 1), (1, 0)])
 
     blocks = {0: own}
     for d in (1, 3, 2):
         blocks[d] = from_x(d)
-    others = {d: from_core(d) for d in (0, 1, 3, 2)}
+    other_0 = from_core(blocks[0])
+    other_3 = from_core(blocks[3])
     columns, ranks = first_moment.shape
-    one = jax.ShapeDtypeStruct((columns, ranks), jnp.bfloat16)
+    two = jax.ShapeDtypeStruct((2, columns, ranks // 2), jnp.bfloat16)
+    eight = jax.ShapeDtypeStruct((8, columns, ranks // 2), jnp.bfloat16)
     four = jax.ShapeDtypeStruct((4, columns, ranks), jnp.bfloat16)
     held = jax.ShapeDtypeStruct((columns, ranks), jnp.float32)
-    part_0 = call(first_block, one, grad, blocks[0], others[0])
-    part_1, part_3 = call(
-        middle_blocks, (one, one), grad, blocks[1], others[1], blocks[3], others[3]
-    )
-    parts = call(last_block, four, grad, blocks[2], others[2], part_0, part_1, part_3)
-    received = exchange(parts)
+    swapped = lax.ppermute(grad, "c", [(0, 1), (1, 0)])
+    parts_0 = call(first_block, two, grad, swapped, blocks[0])
+    parts_3 = call(middle_block, two, grad, swapped, blocks[3])
+    parts, pair = pl.pallas_call(
+        last_blocks,
+        out_shape=(eight, jax.ShapeDtypeStruct((256, grad.shape[1]), jnp.bfloat16)),
+        in_specs=[VMEM] * 6,
+        out_specs=(VMEM,) * 2,
+        scratch_shapes=[pltpu.VMEM((2, columns, ranks), jnp.bfloat16)],
+        compiler_params=limit(8),
+        name="last_blocks",
+    )(grad, swapped, blocks[1], blocks[2], parts_0, parts_3)
+    other_pair = from_core(pair)
+    received = exchange_both(parts)
     first_new, second_new, copies = call(
         moments, (held, held, four), received, first_moment, second_moment
     )
@@ -154,12 +186,12 @@
     return pl.pallas_call(
         back,
         out_shape=(jax.ShapeDtypeStruct((columns, width), jnp.float32), held, held),
-        in_specs=[VMEM] * 11,
+        in_specs=[VMEM] * 9,
         out_specs=(HBM,) * 3,
         scratch_shapes=[pltpu.VMEM((columns, width), jnp.float32), pltpu.SemaphoreType.DMA((6,))],
         compiler_params=limit(8),
         name="back",
-    )(steps, first_new, second_new, *[half[d] for d in range(4) for half in (blocks, others)])
+    )(steps, first_new, second_new, own, other_0, pair, other_pair, blocks[3], other_3)
 
 
 def solution(mesh):

time: 96 us -> 105 us (1.094)
  the two profiles are of different devices: /device:TPU:6 before, /device:TPU:2 now
where the time goes in v1:
time: 105 us
  blocking collectives  38.6 us (37%)
  starting transfers between devices  28.2 us (27%)
  waiting for transfers between devices  24.5 us (23%)
  Pallas kernels  8.18 us (8%)
  local copies, waits for them, and re-layouts  4.44 us (4%)
    all_gather x1, blocking collectives, step(): own = lax.all_gather(projector_t, 'z', axis=0, tiled=True)  38.6 us
    ppermute x3, waiting for transfers between devices, from_x(): return lax.ppermute(own, 'x', [(x, (x - d) % 4) for x in range(4)])  11.9 us
    ppermute x3, starting transfers between devices, from_x(): return lax.ppermute(own, 'x', [(x, (x - d) % 4) for x in range(4)])  10.5 us
    all_to_all x1, waiting for transfers between devices, exchange(): lax.all_to_all(parts, ('x', 'y'), 0, 0, axis_index_groups=ROTATED, tiled=...  8.75 us
    ppermute x3, starting transfers between devices, from_core(): return lax.ppermute(block, 'c', [(0, 1), (1, 0)])  6.23 us
    all_to_all x1, starting transfers between devices, exchange_both(): lax.all_to_all(parts, ('x', 'c', 'y'), 0, 0, axis_index_groups=BOTH, tile...  5.26 us
    unnamed x14, local copies, waits for them, and re-layouts  4.44 us
    all_to_all x1, starting transfers between devices, exchange(): lax.all_to_all(parts, ('x', 'y'), 0, 0, axis_index_groups=ROTATED, tiled=...  4.32 us
  transfers between devices with their start and end apart: 9, of which 5 were waited for; matrix products, arithmetic and copies ran while one was open for 0% of the time, Pallas kernels for 3%

profile of v1, /device:TPU:2, one launch (start us, length us, event | category | flops | bytes accessed | tf_op | source)
XLA Modules:
  0.0 104.7 jit_solution(9407134934374038372)
XLA Ops:
  0.6 1.9 %collective-permute-start = (bf16[224,2048]{1,0:T(8,128)(2,1)}, bf16[224,2048]{1,0:T(8,128)(2,1)S(1)}, u32[]{:S(2)}, u32[]{:S(2)}) collective-permute-start(bf16[224,2048]{1,0:T(8,128)(2,1)} %own.5), channel_id=1, source_target_pairs={{0,4},{4,0},{1,5},{5,1},{2,6},{6,2},{3,7},{7,3},{8,12},{12,8},{9,1... | collective-permute-start | bytes 2752520 | tf_op jit(solution)/shard_map/ppermute | solution.py:166
  2.6 38.6 %all_gather.3.rows.refs_0_ = bf16[128,2048]{1,0:T(8,128)(2,1)S(1)} all-gather(bf16[8,2048]{1,0:T(8,128)(2,1)} %param.5), channel_id=1, replica_groups=mesh['x'=4,'z'=16,'c'=2,'y'=4] {'z'}, dimensions={0}, use_global_device_ids=true | all-gather | bytes 557056 | tf_op jit(solution)/shard_map/all_gather | solution.py:148
  41.1 3.4 %collective-permute-start.3 = (bf16[128,2048]{1,0:T(8,128)(2,1)S(1)}, bf16[128,2048]{1,0:T(8,128)(2,1)S(1)}, u32[]{:S(2)}, u32[]{:S(2)}) collective-permute-start(bf16[128,2048]{1,0:T(8,128)(2,1)S(1)} %all_gather.3.rows.refs_0_), channel_id=1, source_target_pairs={{0,128},{128,256},{256,384},{384,0},{1,129},{129,257},{257,385},{3... | collective-permute-start | bytes 1572872 | tf_op jit(solution)/shard_map/ppermute | solution.py:151
  44.5 3.0 %collective-permute-start.2 = (bf16[128,2048]{1,0:T(8,128)(2,1)S(1)}, bf16[128,2048]{1,0:T(8,128)(2,1)S(1)}, u32[]{:S(2)}, u32[]{:S(2)}) collective-permute-start(bf16[128,2048]{1,0:T(8,128)(2,1)S(1)} %all_gather.3.rows.refs_0_), channel_id=1, source_target_pairs={{0,256},{128,384},{256,0},{384,128},{1,257},{129,385},{257,1},{385... | collective-permute-start | bytes 1572872 | tf_op jit(solution)/shard_map/ppermute | solution.py:151
  47.6 4.1 %collective-permute-start.1 = (bf16[128,2048]{1,0:T(8,128)(2,1)S(1)}, bf16[128,2048]{1,0:T(8,128)(2,1)S(1)}, u32[]{:S(2)}, u32[]{:S(2)}) collective-permute-start(bf16[128,2048]{1,0:T(8,128)(2,1)S(1)} %all_gather.3.rows.refs_0_), channel_id=1, source_target_pairs={{0,384},{128,0},{256,128},{384,256},{1,385},{129,1},{257,129},{385... | collective-permute-start | bytes 1572872 | tf_op jit(solution)/shard_map/ppermute | solution.py:151
  51.7 1.2 %copy-done = bf16[224,2048]{1,0:T(8,128)(2,1)S(1)} copy-done((bf16[224,2048]{1,0:T(8,128)(2,1)S(1)}, bf16[224,2048]{1,0:T(8,128)(2,1)}, u32[]{:S(2)}) %copy-start) | copy-done | bytes 917528
  52.8 0.6 shard_map.67.parts_0
  53.5 2.4 %collective-permute-done.3.rows.refs_4_ = bf16[128,2048]{1,0:T(8,128)(2,1)S(1)} collective-permute-done((bf16[128,2048]{1,0:T(8,128)(2,1)S(1)}, bf16[128,2048]{1,0:T(8,128)(2,1)S(1)}, u32[]{:S(2)}, u32[]{:S(2)}) %collective-permute-start.3) | collective-permute-done | bytes 524320 | tf_op jit(solution)/shard_map/ppermute | solution.py:151
  56.5 4.1 %collective-permute-done.2.rows_2 = bf16[128,2048]{1,0:T(8,128)(2,1)S(1)} collective-permute-done((bf16[128,2048]{1,0:T(8,128)(2,1)S(1)}, bf16[128,2048]{1,0:T(8,128)(2,1)S(1)}, u32[]{:S(2)}, u32[]{:S(2)}) %collective-permute-start.2) | collective-permute-done | bytes 524320 | tf_op jit(solution)/shard_map/ppermute | solution.py:151
  60.6 5.5 %collective-permute-done.1.rows_1 = bf16[128,2048]{1,0:T(8,128)(2,1)S(1)} collective-permute-done((bf16[128,2048]{1,0:T(8,128)(2,1)S(1)}, bf16[128,2048]{1,0:T(8,128)(2,1)S(1)}, u32[]{:S(2)}, u32[]{:S(2)}) %collective-permute-start.1) | collective-permute-done | bytes 524320 | tf_op jit(solution)/shard_map/ppermute | solution.py:151
  66.1 1.7 %last_blocks.1 = (bf16[8,224,128]{2,1,0:T(8,128)(2,1)}, bf16[256,2048]{1,0:T(8,128)(2,1)S(1)}) custom-call(bf16[224,2048]{1,0:T(8,128)(2,1)S(1)} %copy-done, bf16[224,2048]{1,0:T(8,128)(2,1)S(1)} %collective-permute-done.swapped, bf16[128,2048]{1,0:T(8,128)(2,1)S(1)} %collective-permute-done.1.rows_1, bf16[128,2048]{1,0:T(8,128)(2,1)S(1)} %collective-permute-done.2.rows_2, ...), custom_call_target="tpu_custom_call" | custom-call | tf_op jit(solution)/shard_map/last_blocks/pallas_call | solution.py:169
  67.8 1.9 %collective-permute-start.5 = (bf16[256,2048]{1,0:T(8,128)(2,1)S(1)}, bf16[256,2048]{1,0:T(8,128)(2,1)}, u32[]{:S(2)}, u32[]{:S(2)}) collective-permute-start(bf16[256,2048]{1,0:T(8,128)(2,1)S(1)} %get-tuple-element.12.refs_2_), channel_id=1, source_target_pairs={{0,4},{4,0},{1,5},{5,1},{2,6},{6,2},{3,7},{7,3},{8,12},{12,8},{9,1... | collective-permute-start | bytes 3145736 | tf_op jit(solution)/shard_map/ppermute | solution.py:154
  69.7 5.3 %all-to-all-start = ((bf16[8,224,128]{2,1,0:T(8,128)(2,1)}), bf16[8,224,128]{2,1,0:T(8,128)(2,1)S(1)}, u32[]{:S(2)}, u32[]{:S(2)}) async-start(bf16[8,224,128]{2,1,0:T(8,128)(2,1)} %get-tuple-element.8), calls=%async_computation | async-start | bytes 917504 | tf_op jit(solution)/shard_map/all_to_all | solution.py:22
  74.9 2.0 %collective-permute-start.4 = (bf16[128,2048]{1,0:T(8,128)(2,1)S(1)}, bf16[128,2048]{1,0:T(8,128)(2,1)S(1)}, u32[]{:S(2)}, u32[]{:S(2)}) collective-permute-start(bf16[128,2048]{1,0:T(8,128)(2,1)S(1)} %all_gather.3.rows.refs_0_), channel_id=1, source_target_pairs={{0,4},{4,0},{1,5},{5,1},{2,6},{6,2},{3,7},{7,3},{8,12},{12,8},{9,1... | collective-permute-start | bytes 1572872 | tf_op jit(solution)/shard_map/ppermute | solution.py:154
  77.0 2.3 %collective-permute-start.6 = (bf16[128,2048]{1,0:T(8,128)(2,1)S(1)}, bf16[128,2048]{1,0:T(8,128)(2,1)}, u32[]{:S(2)}, u32[]{:S(2)}) collective-permute-start(bf16[128,2048]{1,0:T(8,128)(2,1)S(1)} %collective-permute-done.3.rows.refs_4_), channel_id=1, source_target_pairs={{0,4},{4,0},{1,5},{5,1},{2,6},{6,2},{3,7},{7,3},{8,12},{12,8},{9,1... | collective-permute-start | bytes 1572872 | tf_op jit(solution)/shard_map/ppermute | solution.py:154
  79.3 3.8 %all-to-all-done.received = bf16[8,224,128]{2,1,0:T(8,128)(2,1)S(1)} async-done(((bf16[8,224,128]{2,1,0:T(8,128)(2,1)}), bf16[8,224,128]{2,1,0:T(8,128)(2,1)S(1)}, u32[]{:S(2)}, u32[]{:S(2)}) %all-to-all-start) | async-done | bytes 458784 | tf_op jit(solution)/shard_map/all_to_all | solution.py:22
  83.1 1.9 %shard_map.69 = (f32[224,256]{1,0:T(8,128)S(1)}, f32[224,256]{1,0:T(8,128)S(1)}, bf16[4,224,256]{2,1,0:T(8,128)(2,1)}) custom-call(bf16[8,224,128]{2,1,0:T(8,128)(2,1)S(1)} %all-to-all-done.received, f32[224,256]{1,0:T(8,128)S(1)} %copy-done.1, f32[224,256]{1,0:T(8,128)S(1)} %copy-done.2), custom_call_target="tpu_custom_call" | custom-call | tf_op jit(solution)/shard_map/pallas_call | solution.py:138
  85.0 0.7 copy-done.3
  85.7 0.7 copy-done.5
  86.4 4.3 %all-to-all-start.1 = ((bf16[4,224,256]{2,1,0:T(8,128)(2,1)}), bf16[4,224,256]{2,1,0:T(8,128)(2,1)S(1)}, u32[]{:S(2)}, u32[]{:S(2)}) async-start(bf16[4,224,256]{2,1,0:T(8,128)(2,1)} %get-tuple-element.9), calls=%async_computation.1 | async-start | bytes 917504 | tf_op jit(solution)/shard_map/all_to_all | solution.py:18
  90.7 8.8 %all-to-all-done.1.steps = bf16[4,224,256]{2,1,0:T(8,128)(2,1)S(1)} async-done(((bf16[4,224,256]{2,1,0:T(8,128)(2,1)}), bf16[4,224,256]{2,1,0:T(8,128)(2,1)S(1)}, u32[]{:S(2)}, u32[]{:S(2)}) %all-to-all-start.1) | async-done | bytes 458784 | tf_op jit(solution)/shard_map/all_to_all | solution.py:18
  99.5 0.9 copy-done.4
  100.4 0.9 copy-done.6
  101.4 3.3 %back.1 = (f32[224,2048]{1,0:T(8,128)}, f32[224,256]{1,0:T(8,128)}, f32[224,256]{1,0:T(8,128)}) custom-call(bf16[4,224,256]{2,1,0:T(8,128)(2,1)S(1)} %all-to-all-done.1.steps, f32[224,256]{1,0:T(8,128)S(1)} %copy-done.4, f32[224,256]{1,0:T(8,128)S(1)} %copy-done.6, bf16[128,2048]{1,0:T(8,128)(2,1)S(1)} %all_gather.3.rows.refs_0_, ...), custom_call_target="tpu_custom_call" | custom-call | tf_op jit(solution)/shard_map/back/pallas_call | solution.py:186
  (14 shorter events, 0.7 us)
Async XLA Ops:
  0.6 51.0 %collective-permute-start = (bf16[224,2048]{1,0:T(8,128)(2,1)}, bf16[224,2048]{1,0:T(8,128)(2,1)S(1)}, u32[]{:S(2)}, u32[]{:S(2)}) collective-permute-start(bf16[224,2048]{1,0:T(8,128)(2,1)} %own.5), channel_id=1, source_target_pairs={{0,4},{4,0},{1,5},{5,1},{2,6},{6,2},{3,7},{7,3},{8,12},{12,8},{9,1... | collective-permute-start | bytes 2752520 | tf_op jit(solution)/shard_map/ppermute | solution.py:166
  41.1 14.7 %collective-permute-start.3 = (bf16[128,2048]{1,0:T(8,128)(2,1)S(1)}, bf16[128,2048]{1,0:T(8,128)(2,1)S(1)}, u32[]{:S(2)}, u32[]{:S(2)}) collective-permute-start(bf16[128,2048]{1,0:T(8,128)(2,1)S(1)} %all_gather.3.rows.refs_0_), channel_id=1, source_target_pairs={{0,128},{128,256},{256,384},{384,0},{1,129},{129,257},{257,385},{3... | collective-permute-start | bytes 1572872 | tf_op jit(solution)/shard_map/ppermute | solution.py:151
  44.5 16.1 %collective-permute-start.2 = (bf16[128,2048]{1,0:T(8,128)(2,1)S(1)}, bf16[128,2048]{1,0:T(8,128)(2,1)S(1)}, u32[]{:S(2)}, u32[]{:S(2)}) collective-permute-start(bf16[128,2048]{1,0:T(8,128)(2,1)S(1)} %all_gather.3.rows.refs_0_), channel_id=1, source_target_pairs={{0,256},{128,384},{256,0},{384,128},{1,257},{129,385},{257,1},{385... | collective-permute-start | bytes 1572872 | tf_op jit(solution)/shard_map/ppermute | solution.py:151
  47.6 18.5 %collective-permute-start.1 = (bf16[128,2048]{1,0:T(8,128)(2,1)S(1)}, bf16[128,2048]{1,0:T(8,128)(2,1)S(1)}, u32[]{:S(2)}, u32[]{:S(2)}) collective-permute-start(bf16[128,2048]{1,0:T(8,128)(2,1)S(1)} %all_gather.3.rows.refs_0_), channel_id=1, source_target_pairs={{0,384},{128,0},{256,128},{384,256},{1,385},{129,1},{257,129},{385... | collective-permute-start | bytes 1572872 | tf_op jit(solution)/shard_map/ppermute | solution.py:151
  51.6 1.2 %copy-start = (bf16[224,2048]{1,0:T(8,128)(2,1)S(1)}, bf16[224,2048]{1,0:T(8,128)(2,1)}, u32[]{:S(2)}) copy-start(bf16[224,2048]{1,0:T(8,128)(2,1)} %own.5) | copy-start | bytes 2752516
  56.5 26.6 %copy-start.1 = (f32[224,256]{1,0:T(8,128)S(1)}, f32[224,256]{1,0:T(8,128)}, u32[]{:S(2)}) copy-start(f32[224,256]{1,0:T(8,128)} %first.1) | copy-start | bytes 688132
  56.5 26.6 %copy-start.2 = (f32[224,256]{1,0:T(8,128)S(1)}, f32[224,256]{1,0:T(8,128)}, u32[]{:S(2)}) copy-start(f32[224,256]{1,0:T(8,128)} %second.1) | copy-start | bytes 688132
  67.8 31.7 %collective-permute-start.5 = (bf16[256,2048]{1,0:T(8,128)(2,1)S(1)}, bf16[256,2048]{1,0:T(8,128)(2,1)}, u32[]{:S(2)}, u32[]{:S(2)}) collective-permute-start(bf16[256,2048]{1,0:T(8,128)(2,1)S(1)} %get-tuple-element.12.refs_2_), channel_id=1, source_target_pairs={{0,4},{4,0},{1,5},{5,1},{2,6},{6,2},{3,7},{7,3},{8,12},{12,8},{9,1... | collective-permute-start | bytes 3145736 | tf_op jit(solution)/shard_map/ppermute | solution.py:154
  69.7 13.4 %all-to-all-start = ((bf16[8,224,128]{2,1,0:T(8,128)(2,1)}), bf16[8,224,128]{2,1,0:T(8,128)(2,1)S(1)}, u32[]{:S(2)}, u32[]{:S(2)}) async-start(bf16[8,224,128]{2,1,0:T(8,128)(2,1)} %get-tuple-element.8), calls=%async_computation | async-start | bytes 917504 | tf_op jit(solution)/shard_map/all_to_all | solution.py:22
  74.9 15.8 %collective-permute-start.4 = (bf16[128,2048]{1,0:T(8,128)(2,1)S(1)}, bf16[128,2048]{1,0:T(8,128)(2,1)S(1)}, u32[]{:S(2)}, u32[]{:S(2)}) collective-permute-start(bf16[128,2048]{1,0:T(8,128)(2,1)S(1)} %all_gather.3.rows.refs_0_), channel_id=1, source_target_pairs={{0,4},{4,0},{1,5},{5,1},{2,6},{6,2},{3,7},{7,3},{8,12},{12,8},{9,1... | collective-permute-start | bytes 1572872 | tf_op jit(solution)/shard_map/ppermute | solution.py:154
  77.0 13.8 %collective-permute-start.6 = (bf16[128,2048]{1,0:T(8,128)(2,1)S(1)}, bf16[128,2048]{1,0:T(8,128)(2,1)}, u32[]{:S(2)}, u32[]{:S(2)}) collective-permute-start(bf16[128,2048]{1,0:T(8,128)(2,1)S(1)} %collective-permute-done.3.rows.refs_4_), channel_id=1, source_target_pairs={{0,4},{4,0},{1,5},{5,1},{2,6},{6,2},{3,7},{7,3},{8,12},{12,8},{9,1... | collective-permute-start | bytes 1572872 | tf_op jit(solution)/shard_map/ppermute | solution.py:154
  85.0 0.7 copy-start.3
  85.7 0.7 copy-start.5
  86.4 13.1 %all-to-all-start.1 = ((bf16[4,224,256]{2,1,0:T(8,128)(2,1)}), bf16[4,224,256]{2,1,0:T(8,128)(2,1)S(1)}, u32[]{:S(2)}, u32[]{:S(2)}) async-start(bf16[4,224,256]{2,1,0:T(8,128)(2,1)} %get-tuple-element.9), calls=%async_computation.1 | async-start | bytes 917504 | tf_op jit(solution)/shard_map/all_to_all | solution.py:18
  99.5 0.9 copy-start.4
  100.4 0.9 copy-start.6

commit v2 on v1

--- a/solution.py
+++ b/solution.py
@@ -11,7 +11,7 @@
 FSDP = ("x", "z", "c")
 VMEM = pl.BlockSpec(memory_space=pltpu.VMEM)
 ROTATED = [[4 * x + (x + d) % 4 for d in range(4)] for x in range(4)]
-BOTH = [[(2 * x + c) * 4 + (x + d) % 4 for c in range(2) for d in range(4)] for x in range(4)]
+BOTH = [[(2 * x + c) * 4 + (x + d) % 4 for d in range(4) for c in range(2)] for x in range(4)]
 
 
 def exchange(parts):
@@ -57,11 +57,11 @@
     pair[...] = rows
     project(own, swapped, rows, held)
     for k in range(2):
-        slot = 4 * jnp.bitwise_xor(core, k)
+        slot = jnp.bitwise_xor(core, k)
         out[slot] = parts_0[k]
-        out[slot + 1] = held[k, :, :128]
-        out[slot + 2] = held[k, :, 128:]
-        out[slot + 3] = parts_3[k]
+        out[slot + 2] = held[k, :, :128]
+        out[slot + 4] = held[k, :, 128:]
+        out[slot + 6] = parts_3[k]
 
 
 def moments(received, first, second, first_out, second_out, copies):
@@ -73,8 +73,8 @@
     place = (rank == spot).astype(jnp.bfloat16)
     halves = []
     for k in range(2):
-        slot = 4 * jnp.bitwise_xor(core, k)
-        halves.append(sum(decode(received[slot + d]) for d in range(4)))
+        slot = jnp.bitwise_xor(core, k)
+        halves.append(sum(decode(received[slot + 2 * d]) for d in range(4)))
     left = jnp.concatenate(halves, axis=1)
     projected = jnp.zeros(first.shape, jnp.float32)
     for _ in range(3):

time: 105 us -> 105 us (level)
  no operation moved by 1% of the time
where the time goes in v2:
time: 105 us; the launch traced here: 104 us
  blocking collectives  38.6 us (37%)
  starting transfers between devices  28.8 us (27%)
  waiting for transfers between devices  23.7 us (23%)
  Pallas kernels  8.18 us (8%)
  local copies, waits for them, and re-layouts  4.44 us (4%)
    all_gather x1, blocking collectives, step(): own = lax.all_gather(projector_t, 'z', axis=0, tiled=True)  38.6 us
    ppermute x3, waiting for transfers between devices, from_x(): return lax.ppermute(own, 'x', [(x, (x - d) % 4) for x in range(4)])  11.9 us
    ppermute x3, starting transfers between devices, from_x(): return lax.ppermute(own, 'x', [(x, (x - d) % 4) for x in range(4)])  10.5 us
    all_to_all x1, waiting for transfers between devices, exchange(): lax.all_to_all(parts, ('x', 'y'), 0, 0, axis_index_groups=ROTATED, tiled=...  7.89 us
    ppermute x3, starting transfers between devices, from_core(): return lax.ppermute(block, 'c', [(0, 1), (1, 0)])  6.23 us
    all_to_all x1, starting transfers between devices, exchange_both(): lax.all_to_all(parts, ('x', 'c', 'y'), 0, 0, axis_index_groups=BOTH, tile...  5.26 us
    all_to_all x1, starting transfers between devices, exchange(): lax.all_to_all(parts, ('x', 'y'), 0, 0, axis_index_groups=ROTATED, tiled=...  4.89 us
    unnamed x14, local copies, waits for them, and re-layouts  4.44 us
  transfers between devices with their start and end apart: 9, of which 5 were waited for; matrix products, arithmetic and copies ran while one was open for 0% of the time, Pallas kernels for 3%

profile of v2, /device:TPU:2, one launch (start us, length us, event | category | flops | bytes accessed | tf_op | source)
XLA Modules:
  0.0 104.4 jit_solution(3001194464403544507)
XLA Ops:
  0.6 1.9 %collective-permute-start = (bf16[224,2048]{1,0:T(8,128)(2,1)}, bf16[224,2048]{1,0:T(8,128)(2,1)S(1)}, u32[]{:S(2)}, u32[]{:S(2)}) collective-permute-start(bf16[224,2048]{1,0:T(8,128)(2,1)} %own.5), channel_id=1, source_target_pairs={{0,4},{4,0},{1,5},{5,1},{2,6},{6,2},{3,7},{7,3},{8,12},{12,8},{9,1... | collective-permute-start | bytes 2752520 | tf_op jit(solution)/shard_map/ppermute | solution.py:166
  2.6 38.6 %all_gather.3.rows.refs_0_ = bf16[128,2048]{1,0:T(8,128)(2,1)S(1)} all-gather(bf16[8,2048]{1,0:T(8,128)(2,1)} %param.5), channel_id=1, replica_groups=mesh['x'=4,'z'=16,'c'=2,'y'=4] {'z'}, dimensions={0}, use_global_device_ids=true | all-gather | bytes 557056 | tf_op jit(solution)/shard_map/all_gather | solution.py:148
  41.1 3.4 %collective-permute-start.3 = (bf16[128,2048]{1,0:T(8,128)(2,1)S(1)}, bf16[128,2048]{1,0:T(8,128)(2,1)S(1)}, u32[]{:S(2)}, u32[]{:S(2)}) collective-permute-start(bf16[128,2048]{1,0:T(8,128)(2,1)S(1)} %all_gather.3.rows.refs_0_), channel_id=1, source_target_pairs={{0,128},{128,256},{256,384},{384,0},{1,129},{129,257},{257,385},{3... | collective-permute-start | bytes 1572872 | tf_op jit(solution)/shard_map/ppermute | solution.py:151
  44.5 3.0 %collective-permute-start.2 = (bf16[128,2048]{1,0:T(8,128)(2,1)S(1)}, bf16[128,2048]{1,0:T(8,128)(2,1)S(1)}, u32[]{:S(2)}, u32[]{:S(2)}) collective-permute-start(bf16[128,2048]{1,0:T(8,128)(2,1)S(1)} %all_gather.3.rows.refs_0_), channel_id=1, source_target_pairs={{0,256},{128,384},{256,0},{384,128},{1,257},{129,385},{257,1},{385... | collective-permute-start | bytes 1572872 | tf_op jit(solution)/shard_map/ppermute | solution.py:151
  47.6 4.1 %collective-permute-start.1 = (bf16[128,2048]{1,0:T(8,128)(2,1)S(1)}, bf16[128,2048]{1,0:T(8,128)(2,1)S(1)}, u32[]{:S(2)}, u32[]{:S(2)}) collective-permute-start(bf16[128,2048]{1,0:T(8,128)(2,1)S(1)} %all_gather.3.rows.refs_0_), channel_id=1, source_target_pairs={{0,384},{128,0},{256,128},{384,256},{1,385},{129,1},{257,129},{385... | collective-permute-start | bytes 1572872 | tf_op jit(solution)/shard_map/ppermute | solution.py:151
  51.7 1.2 %copy-done = bf16[224,2048]{1,0:T(8,128)(2,1)S(1)} copy-done((bf16[224,2048]{1,0:T(8,128)(2,1)S(1)}, bf16[224,2048]{1,0:T(8,128)(2,1)}, u32[]{:S(2)}) %copy-start) | copy-done | bytes 917528
  52.8 0.6 shard_map.67.parts_0
  53.5 2.4 %collective-permute-done.3.rows.refs_4_ = bf16[128,2048]{1,0:T(8,128)(2,1)S(1)} collective-permute-done((bf16[128,2048]{1,0:T(8,128)(2,1)S(1)}, bf16[128,2048]{1,0:T(8,128)(2,1)S(1)}, u32[]{:S(2)}, u32[]{:S(2)}) %collective-permute-start.3) | collective-permute-done | bytes 524320 | tf_op jit(solution)/shard_map/ppermute | solution.py:151
  56.5 4.1 %collective-permute-done.2.rows_2 = bf16[128,2048]{1,0:T(8,128)(2,1)S(1)} collective-permute-done((bf16[128,2048]{1,0:T(8,128)(2,1)S(1)}, bf16[128,2048]{1,0:T(8,128)(2,1)S(1)}, u32[]{:S(2)}, u32[]{:S(2)}) %collective-permute-start.2) | collective-permute-done | bytes 524320 | tf_op jit(solution)/shard_map/ppermute | solution.py:151
  60.6 5.5 %collective-permute-done.1.rows_1 = bf16[128,2048]{1,0:T(8,128)(2,1)S(1)} collective-permute-done((bf16[128,2048]{1,0:T(8,128)(2,1)S(1)}, bf16[128,2048]{1,0:T(8,128)(2,1)S(1)}, u32[]{:S(2)}, u32[]{:S(2)}) %collective-permute-start.1) | collective-permute-done | bytes 524320 | tf_op jit(solution)/shard_map/ppermute | solution.py:151
  66.1 1.7 %last_blocks.1 = (bf16[8,224,128]{2,1,0:T(8,128)(2,1)}, bf16[256,2048]{1,0:T(8,128)(2,1)S(1)}) custom-call(bf16[224,2048]{1,0:T(8,128)(2,1)S(1)} %copy-done, bf16[224,2048]{1,0:T(8,128)(2,1)S(1)} %collective-permute-done.swapped, bf16[128,2048]{1,0:T(8,128)(2,1)S(1)} %collective-permute-done.1.rows_1, bf16[128,2048]{1,0:T(8,128)(2,1)S(1)} %collective-permute-done.2.rows_2, ...), custom_call_target="tpu_custom_call" | custom-call | tf_op jit(solution)/shard_map/last_blocks/pallas_call | solution.py:169
  67.8 1.9 %collective-permute-start.5 = (bf16[256,2048]{1,0:T(8,128)(2,1)S(1)}, bf16[256,2048]{1,0:T(8,128)(2,1)}, u32[]{:S(2)}, u32[]{:S(2)}) collective-permute-start(bf16[256,2048]{1,0:T(8,128)(2,1)S(1)} %get-tuple-element.12.refs_2_), channel_id=1, source_target_pairs={{0,4},{4,0},{1,5},{5,1},{2,6},{6,2},{3,7},{7,3},{8,12},{12,8},{9,1... | collective-permute-start | bytes 3145736 | tf_op jit(solution)/shard_map/ppermute | solution.py:154
  69.7 5.3 %all-to-all-start = ((bf16[8,224,128]{2,1,0:T(8,128)(2,1)}), bf16[8,224,128]{2,1,0:T(8,128)(2,1)S(1)}, u32[]{:S(2)}, u32[]{:S(2)}) async-start(bf16[8,224,128]{2,1,0:T(8,128)(2,1)} %get-tuple-element.8), calls=%async_computation | async-start | bytes 917504 | tf_op jit(solution)/shard_map/all_to_all | solution.py:22
  74.9 2.0 %collective-permute-start.4 = (bf16[128,2048]{1,0:T(8,128)(2,1)S(1)}, bf16[128,2048]{1,0:T(8,128)(2,1)S(1)}, u32[]{:S(2)}, u32[]{:S(2)}) collective-permute-start(bf16[128,2048]{1,0:T(8,128)(2,1)S(1)} %all_gather.3.rows.refs_0_), channel_id=1, source_target_pairs={{0,4},{4,0},{1,5},{5,1},{2,6},{6,2},{3,7},{7,3},{8,12},{12,8},{9,1... | collective-permute-start | bytes 1572872 | tf_op jit(solution)/shard_map/ppermute | solution.py:154
  77.0 2.3 %collective-permute-start.6 = (bf16[128,2048]{1,0:T(8,128)(2,1)S(1)}, bf16[128,2048]{1,0:T(8,128)(2,1)}, u32[]{:S(2)}, u32[]{:S(2)}) collective-permute-start(bf16[128,2048]{1,0:T(8,128)(2,1)S(1)} %collective-permute-done.3.rows.refs_4_), channel_id=1, source_target_pairs={{0,4},{4,0},{1,5},{5,1},{2,6},{6,2},{3,7},{7,3},{8,12},{12,8},{9,1... | collective-permute-start | bytes 1572872 | tf_op jit(solution)/shard_map/ppermute | solution.py:154
  79.3 3.8 %all-to-all-done.received = bf16[8,224,128]{2,1,0:T(8,128)(2,1)S(1)} async-done(((bf16[8,224,128]{2,1,0:T(8,128)(2,1)}), bf16[8,224,128]{2,1,0:T(8,128)(2,1)S(1)}, u32[]{:S(2)}, u32[]{:S(2)}) %all-to-all-start) | async-done | bytes 458784 | tf_op jit(solution)/shard_map/all_to_all | solution.py:22
  83.1 1.9 %shard_map.69 = (f32[224,256]{1,0:T(8,128)S(1)}, f32[224,256]{1,0:T(8,128)S(1)}, bf16[4,224,256]{2,1,0:T(8,128)(2,1)}) custom-call(bf16[8,224,128]{2,1,0:T(8,128)(2,1)S(1)} %all-to-all-done.received, f32[224,256]{1,0:T(8,128)S(1)} %copy-done.1, f32[224,256]{1,0:T(8,128)S(1)} %copy-done.2), custom_call_target="tpu_custom_call" | custom-call | tf_op jit(solution)/shard_map/pallas_call | solution.py:138
  85.0 0.7 copy-done.3
  85.7 0.7 copy-done.5
  86.4 4.9 %all-to-all-start.1 = ((bf16[4,224,256]{2,1,0:T(8,128)(2,1)}), bf16[4,224,256]{2,1,0:T(8,128)(2,1)S(1)}, u32[]{:S(2)}, u32[]{:S(2)}) async-start(bf16[4,224,256]{2,1,0:T(8,128)(2,1)} %get-tuple-element.9), calls=%async_computation.1 | async-start | bytes 917504 | tf_op jit(solution)/shard_map/all_to_all | solution.py:18
  91.3 7.9 %all-to-all-done.1.steps = bf16[4,224,256]{2,1,0:T(8,128)(2,1)S(1)} async-done(((bf16[4,224,256]{2,1,0:T(8,128)(2,1)}), bf16[4,224,256]{2,1,0:T(8,128)(2,1)S(1)}, u32[]{:S(2)}, u32[]{:S(2)}) %all-to-all-start.1) | async-done | bytes 458784 | tf_op jit(solution)/shard_map/all_to_all | solution.py:18
  99.2 0.9 copy-done.4
  100.2 0.9 copy-done.6
  101.1 3.3 %back.1 = (f32[224,2048]{1,0:T(8,128)}, f32[224,256]{1,0:T(8,128)}, f32[224,256]{1,0:T(8,128)}) custom-call(bf16[4,224,256]{2,1,0:T(8,128)(2,1)S(1)} %all-to-all-done.1.steps, f32[224,256]{1,0:T(8,128)S(1)} %copy-done.4, f32[224,256]{1,0:T(8,128)S(1)} %copy-done.6, bf16[128,2048]{1,0:T(8,128)(2,1)S(1)} %all_gather.3.rows.refs_0_, ...), custom_call_target="tpu_custom_call" | custom-call | tf_op jit(solution)/shard_map/back/pallas_call | solution.py:186
  (14 shorter events, 0.7 us)
Async XLA Ops:
  0.6 51.0 %collective-permute-start = (bf16[224,2048]{1,0:T(8,128)(2,1)}, bf16[224,2048]{1,0:T(8,128)(2,1)S(1)}, u32[]{:S(2)}, u32[]{:S(2)}) collective-permute-start(bf16[224,2048]{1,0:T(8,128)(2,1)} %own.5), channel_id=1, source_target_pairs={{0,4},{4,0},{1,5},{5,1},{2,6},{6,2},{3,7},{7,3},{8,12},{12,8},{9,1... | collective-permute-start | bytes 2752520 | tf_op jit(solution)/shard_map/ppermute | solution.py:166
  41.1 14.7 %collective-permute-start.3 = (bf16[128,2048]{1,0:T(8,128)(2,1)S(1)}, bf16[128,2048]{1,0:T(8,128)(2,1)S(1)}, u32[]{:S(2)}, u32[]{:S(2)}) collective-permute-start(bf16[128,2048]{1,0:T(8,128)(2,1)S(1)} %all_gather.3.rows.refs_0_), channel_id=1, source_target_pairs={{0,128},{128,256},{256,384},{384,0},{1,129},{129,257},{257,385},{3... | collective-permute-start | bytes 1572872 | tf_op jit(solution)/shard_map/ppermute | solution.py:151
  44.5 16.1 %collective-permute-start.2 = (bf16[128,2048]{1,0:T(8,128)(2,1)S(1)}, bf16[128,2048]{1,0:T(8,128)(2,1)S(1)}, u32[]{:S(2)}, u32[]{:S(2)}) collective-permute-start(bf16[128,2048]{1,0:T(8,128)(2,1)S(1)} %all_gather.3.rows.refs_0_), channel_id=1, source_target_pairs={{0,256},{128,384},{256,0},{384,128},{1,257},{129,385},{257,1},{385... | collective-permute-start | bytes 1572872 | tf_op jit(solution)/shard_map/ppermute | solution.py:151
  47.6 18.5 %collective-permute-start.1 = (bf16[128,2048]{1,0:T(8,128)(2,1)S(1)}, bf16[128,2048]{1,0:T(8,128)(2,1)S(1)}, u32[]{:S(2)}, u32[]{:S(2)}) collective-permute-start(bf16[128,2048]{1,0:T(8,128)(2,1)S(1)} %all_gather.3.rows.refs_0_), channel_id=1, source_target_pairs={{0,384},{128,0},{256,128},{384,256},{1,385},{129,1},{257,129},{385... | collective-permute-start | bytes 1572872 | tf_op jit(solution)/shard_map/ppermute | solution.py:151
  51.6 1.2 %copy-start = (bf16[224,2048]{1,0:T(8,128)(2,1)S(1)}, bf16[224,2048]{1,0:T(8,128)(2,1)}, u32[]{:S(2)}) copy-start(bf16[224,2048]{1,0:T(8,128)(2,1)} %own.5) | copy-start | bytes 2752516
  56.5 26.6 %copy-start.1 = (f32[224,256]{1,0:T(8,128)S(1)}, f32[224,256]{1,0:T(8,128)}, u32[]{:S(2)}) copy-start(f32[224,256]{1,0:T(8,128)} %first.1) | copy-start | bytes 688132
  56.5 26.6 %copy-start.2 = (f32[224,256]{1,0:T(8,128)S(1)}, f32[224,256]{1,0:T(8,128)}, u32[]{:S(2)}) copy-start(f32[224,256]{1,0:T(8,128)} %second.1) | copy-start | bytes 688132
  67.8 31.5 %collective-permute-start.5 = (bf16[256,2048]{1,0:T(8,128)(2,1)S(1)}, bf16[256,2048]{1,0:T(8,128)(2,1)}, u32[]{:S(2)}, u32[]{:S(2)}) collective-permute-start(bf16[256,2048]{1,0:T(8,128)(2,1)S(1)} %get-tuple-element.12.refs_2_), channel_id=1, source_target_pairs={{0,4},{4,0},{1,5},{5,1},{2,6},{6,2},{3,7},{7,3},{8,12},{12,8},{9,1... | collective-permute-start | bytes 3145736 | tf_op jit(solution)/shard_map/ppermute | solution.py:154
  69.7 13.4 %all-to-all-start = ((bf16[8,224,128]{2,1,0:T(8,128)(2,1)}), bf16[8,224,128]{2,1,0:T(8,128)(2,1)S(1)}, u32[]{:S(2)}, u32[]{:S(2)}) async-start(bf16[8,224,128]{2,1,0:T(8,128)(2,1)} %get-tuple-element.8), calls=%async_computation | async-start | bytes 917504 | tf_op jit(solution)/shard_map/all_to_all | solution.py:22
  74.9 16.4 %collective-permute-start.4 = (bf16[128,2048]{1,0:T(8,128)(2,1)S(1)}, bf16[128,2048]{1,0:T(8,128)(2,1)S(1)}, u32[]{:S(2)}, u32[]{:S(2)}) collective-permute-start(bf16[128,2048]{1,0:T(8,128)(2,1)S(1)} %all_gather.3.rows.refs_0_), channel_id=1, source_target_pairs={{0,4},{4,0},{1,5},{5,1},{2,6},{6,2},{3,7},{7,3},{8,12},{12,8},{9,1... | collective-permute-start | bytes 1572872 | tf_op jit(solution)/shard_map/ppermute | solution.py:154
  77.0 14.4 %collective-permute-start.6 = (bf16[128,2048]{1,0:T(8,128)(2,1)S(1)}, bf16[128,2048]{1,0:T(8,128)(2,1)}, u32[]{:S(2)}, u32[]{:S(2)}) collective-permute-start(bf16[128,2048]{1,0:T(8,128)(2,1)S(1)} %collective-permute-done.3.rows.refs_4_), channel_id=1, source_target_pairs={{0,4},{4,0},{1,5},{5,1},{2,6},{6,2},{3,7},{7,3},{8,12},{12,8},{9,1... | collective-permute-start | bytes 1572872 | tf_op jit(solution)/shard_map/ppermute | solution.py:154
  85.0 0.7 copy-start.3
  85.7 0.7 copy-start.5
  86.4 12.8 %all-to-all-start.1 = ((bf16[4,224,256]{2,1,0:T(8,128)(2,1)}), bf16[4,224,256]{2,1,0:T(8,128)(2,1)S(1)}, u32[]{:S(2)}, u32[]{:S(2)}) async-start(bf16[4,224,256]{2,1,0:T(8,128)(2,1)} %get-tuple-element.9), calls=%async_computation.1 | async-start | bytes 917504 | tf_op jit(solution)/shard_map/all_to_all | solution.py:18
  99.2 0.9 copy-start.4
  100.2 0.9 copy-start.6

commit v3 on v2

--- a/solution.py
+++ b/solution.py
@@ -71,16 +71,13 @@
     half = jnp.bitwise_xor(lax.shift_right_logical(at, 7), core)
     spot = (lax.shift_right_logical(at, 3) & 15) * 16 + half * 8 + (at & 7)
     place = (rank == spot).astype(jnp.bfloat16)
-    halves = []
-    for k in range(2):
-        slot = jnp.bitwise_xor(core, k)
-        halves.append(sum(decode(received[slot + 2 * d]) for d in range(4)))
-    left = jnp.concatenate(halves, axis=1)
     projected = jnp.zeros(first.shape, jnp.float32)
-    for _ in range(3):
-        piece = left.astype(jnp.bfloat16)
-        projected += jnp.dot(piece, place, preferred_element_type=jnp.float32)
-        left = left - piece.astype(jnp.float32)
+    for d in range(4):
+        both = [received[jnp.bitwise_xor(core, k) + 2 * d] for k in range(2)]
+        moved = jnp.dot(
+            jnp.concatenate(both, axis=1), place, preferred_element_type=jnp.float32
+        )
+        projected += decode(moved)
     first_new = 0.9 * first[...] + 0.1 * projected
     second_new = 0.999 * second[...] + 0.001 * projected * projected
     first_out[...] = first_new

time: 105 us -> 105 us (level)
  no operation moved by 1% of the time
where the time goes in v3:
time: 105 us; the launch traced here: 104 us
  blocking collectives  38.6 us (37%)
  starting transfers between devices  28.8 us (27%)
  waiting for transfers between devices  23.7 us (23%)
  Pallas kernels  8.11 us (8%)
  local copies, waits for them, and re-layouts  4.44 us (4%)
    all_gather x1, blocking collectives, step(): own = lax.all_gather(projector_t, 'z', axis=0, tiled=True)  38.6 us
    ppermute x3, waiting for transfers between devices, from_x(): return lax.ppermute(own, 'x', [(x, (x - d) % 4) for x in range(4)])  11.9 us
    ppermute x3, starting transfers between devices, from_x(): return lax.ppermute(own, 'x', [(x, (x - d) % 4) for x in range(4)])  10.5 us
    all_to_all x1, waiting for transfers between devices, exchange(): lax.all_to_all(parts, ('x', 'y'), 0, 0, axis_index_groups=ROTATED, tiled=...  7.89 us
    ppermute x3, starting transfers between devices, from_core(): return lax.ppermute(block, 'c', [(0, 1), (1, 0)])  6.23 us
    all_to_all x1, starting transfers between devices, exchange_both(): lax.all_to_all(parts, ('x', 'c', 'y'), 0, 0, axis_index_groups=BOTH, tile...  5.26 us
    all_to_all x1, starting transfers between devices, exchange(): lax.all_to_all(parts, ('x', 'y'), 0, 0, axis_index_groups=ROTATED, tiled=...  4.89 us
    unnamed x14, local copies, waits for them, and re-layouts  4.44 us
  transfers between devices with their start and end apart: 9, of which 5 were waited for; matrix products, arithmetic and copies ran while one was open for 0% of the time, Pallas kernels for 3%

profile of v3, /device:TPU:2, one launch (start us, length us, event | category | flops | bytes accessed | tf_op | source)
XLA Modules:
  0.0 104.3 jit_solution(14330974359885645777)
XLA Ops:
  0.6 1.9 %collective-permute-start = (bf16[224,2048]{1,0:T(8,128)(2,1)}, bf16[224,2048]{1,0:T(8,128)(2,1)S(1)}, u32[]{:S(2)}, u32[]{:S(2)}) collective-permute-start(bf16[224,2048]{1,0:T(8,128)(2,1)} %own.5), channel_id=1, source_target_pairs={{0,4},{4,0},{1,5},{5,1},{2,6},{6,2},{3,7},{7,3},{8,12},{12,8},{9,1... | collective-permute-start | bytes 2752520 | tf_op jit(solution)/shard_map/ppermute | solution.py:163
  2.6 38.6 %all_gather.3.rows.refs_0_ = bf16[128,2048]{1,0:T(8,128)(2,1)S(1)} all-gather(bf16[8,2048]{1,0:T(8,128)(2,1)} %param.5), channel_id=1, replica_groups=mesh['x'=4,'z'=16,'c'=2,'y'=4] {'z'}, dimensions={0}, use_global_device_ids=true | all-gather | bytes 557056 | tf_op jit(solution)/shard_map/all_gather | solution.py:145
  41.1 3.4 %collective-permute-start.3 = (bf16[128,2048]{1,0:T(8,128)(2,1)S(1)}, bf16[128,2048]{1,0:T(8,128)(2,1)S(1)}, u32[]{:S(2)}, u32[]{:S(2)}) collective-permute-start(bf16[128,2048]{1,0:T(8,128)(2,1)S(1)} %all_gather.3.rows.refs_0_), channel_id=1, source_target_pairs={{0,128},{128,256},{256,384},{384,0},{1,129},{129,257},{257,385},{3... | collective-permute-start | bytes 1572872 | tf_op jit(solution)/shard_map/ppermute | solution.py:148
  44.5 3.0 %collective-permute-start.2 = (bf16[128,2048]{1,0:T(8,128)(2,1)S(1)}, bf16[128,2048]{1,0:T(8,128)(2,1)S(1)}, u32[]{:S(2)}, u32[]{:S(2)}) collective-permute-start(bf16[128,2048]{1,0:T(8,128)(2,1)S(1)} %all_gather.3.rows.refs_0_), channel_id=1, source_target_pairs={{0,256},{128,384},{256,0},{384,128},{1,257},{129,385},{257,1},{385... | collective-permute-start | bytes 1572872 | tf_op jit(solution)/shard_map/ppermute | solution.py:148
  47.6 4.1 %collective-permute-start.1 = (bf16[128,2048]{1,0:T(8,128)(2,1)S(1)}, bf16[128,2048]{1,0:T(8,128)(2,1)S(1)}, u32[]{:S(2)}, u32[]{:S(2)}) collective-permute-start(bf16[128,2048]{1,0:T(8,128)(2,1)S(1)} %all_gather.3.rows.refs_0_), channel_id=1, source_target_pairs={{0,384},{128,0},{256,128},{384,256},{1,385},{129,1},{257,129},{385... | collective-permute-start | bytes 1572872 | tf_op jit(solution)/shard_map/ppermute | solution.py:148
  51.7 1.2 %copy-done = bf16[224,2048]{1,0:T(8,128)(2,1)S(1)} copy-done((bf16[224,2048]{1,0:T(8,128)(2,1)S(1)}, bf16[224,2048]{1,0:T(8,128)(2,1)}, u32[]{:S(2)}) %copy-start) | copy-done | bytes 917528
  52.8 0.6 shard_map.67.parts_0
  53.5 2.4 %collective-permute-done.3.rows.refs_4_ = bf16[128,2048]{1,0:T(8,128)(2,1)S(1)} collective-permute-done((bf16[128,2048]{1,0:T(8,128)(2,1)S(1)}, bf16[128,2048]{1,0:T(8,128)(2,1)S(1)}, u32[]{:S(2)}, u32[]{:S(2)}) %collective-permute-start.3) | collective-permute-done | bytes 524320 | tf_op jit(solution)/shard_map/ppermute | solution.py:148
  56.5 4.1 %collective-permute-done.2.rows_2 = bf16[128,2048]{1,0:T(8,128)(2,1)S(1)} collective-permute-done((bf16[128,2048]{1,0:T(8,128)(2,1)S(1)}, bf16[128,2048]{1,0:T(8,128)(2,1)S(1)}, u32[]{:S(2)}, u32[]{:S(2)}) %collective-permute-start.2) | collective-permute-done | bytes 524320 | tf_op jit(solution)/shard_map/ppermute | solution.py:148
  60.6 5.5 %collective-permute-done.1.rows_1 = bf16[128,2048]{1,0:T(8,128)(2,1)S(1)} collective-permute-done((bf16[128,2048]{1,0:T(8,128)(2,1)S(1)}, bf16[128,2048]{1,0:T(8,128)(2,1)S(1)}, u32[]{:S(2)}, u32[]{:S(2)}) %collective-permute-start.1) | collective-permute-done | bytes 524320 | tf_op jit(solution)/shard_map/ppermute | solution.py:148
  66.1 1.7 %last_blocks.1 = (bf16[8,224,128]{2,1,0:T(8,128)(2,1)}, bf16[256,2048]{1,0:T(8,128)(2,1)S(1)}) custom-call(bf16[224,2048]{1,0:T(8,128)(2,1)S(1)} %copy-done, bf16[224,2048]{1,0:T(8,128)(2,1)S(1)} %collective-permute-done.swapped, bf16[128,2048]{1,0:T(8,128)(2,1)S(1)} %collective-permute-done.1.rows_1, bf16[128,2048]{1,0:T(8,128)(2,1)S(1)} %collective-permute-done.2.rows_2, ...), custom_call_target="tpu_custom_call" | custom-call | tf_op jit(solution)/shard_map/last_blocks/pallas_call | solution.py:166
  67.8 1.9 %collective-permute-start.5 = (bf16[256,2048]{1,0:T(8,128)(2,1)S(1)}, bf16[256,2048]{1,0:T(8,128)(2,1)}, u32[]{:S(2)}, u32[]{:S(2)}) collective-permute-start(bf16[256,2048]{1,0:T(8,128)(2,1)S(1)} %get-tuple-element.12.refs_2_), channel_id=1, source_target_pairs={{0,4},{4,0},{1,5},{5,1},{2,6},{6,2},{3,7},{7,3},{8,12},{12,8},{9,1... | collective-permute-start | bytes 3145736 | tf_op jit(solution)/shard_map/ppermute | solution.py:151
  69.7 5.3 %all-to-all-start = ((bf16[8,224,128]{2,1,0:T(8,128)(2,1)}), bf16[8,224,128]{2,1,0:T(8,128)(2,1)S(1)}, u32[]{:S(2)}, u32[]{:S(2)}) async-start(bf16[8,224,128]{2,1,0:T(8,128)(2,1)} %get-tuple-element.8), calls=%async_computation | async-start | bytes 917504 | tf_op jit(solution)/shard_map/all_to_all | solution.py:22
  74.9 2.0 %collective-permute-start.4 = (bf16[128,2048]{1,0:T(8,128)(2,1)S(1)}, bf16[128,2048]{1,0:T(8,128)(2,1)S(1)}, u32[]{:S(2)}, u32[]{:S(2)}) collective-permute-start(bf16[128,2048]{1,0:T(8,128)(2,1)S(1)} %all_gather.3.rows.refs_0_), channel_id=1, source_target_pairs={{0,4},{4,0},{1,5},{5,1},{2,6},{6,2},{3,7},{7,3},{8,12},{12,8},{9,1... | collective-permute-start | bytes 1572872 | tf_op jit(solution)/shard_map/ppermute | solution.py:151
  77.0 2.3 %collective-permute-start.6 = (bf16[128,2048]{1,0:T(8,128)(2,1)S(1)}, bf16[128,2048]{1,0:T(8,128)(2,1)}, u32[]{:S(2)}, u32[]{:S(2)}) collective-permute-start(bf16[128,2048]{1,0:T(8,128)(2,1)S(1)} %collective-permute-done.3.rows.refs_4_), channel_id=1, source_target_pairs={{0,4},{4,0},{1,5},{5,1},{2,6},{6,2},{3,7},{7,3},{8,12},{12,8},{9,1... | collective-permute-start | bytes 1572872 | tf_op jit(solution)/shard_map/ppermute | solution.py:151
  79.3 3.8 %all-to-all-done.received = bf16[8,224,128]{2,1,0:T(8,128)(2,1)S(1)} async-done(((bf16[8,224,128]{2,1,0:T(8,128)(2,1)}), bf16[8,224,128]{2,1,0:T(8,128)(2,1)S(1)}, u32[]{:S(2)}, u32[]{:S(2)}) %all-to-all-start) | async-done | bytes 458784 | tf_op jit(solution)/shard_map/all_to_all | solution.py:22
  83.1 1.9 %shard_map.69 = (f32[224,256]{1,0:T(8,128)S(1)}, f32[224,256]{1,0:T(8,128)S(1)}, bf16[4,224,256]{2,1,0:T(8,128)(2,1)}) custom-call(bf16[8,224,128]{2,1,0:T(8,128)(2,1)S(1)} %all-to-all-done.received, f32[224,256]{1,0:T(8,128)S(1)} %copy-done.1, f32[224,256]{1,0:T(8,128)S(1)} %copy-done.2), custom_call_target="tpu_custom_call" | custom-call | tf_op jit(solution)/shard_map/pallas_call | solution.py:135
  85.0 0.7 copy-done.3
  85.7 0.7 copy-done.5
  86.3 4.9 %all-to-all-start.1 = ((bf16[4,224,256]{2,1,0:T(8,128)(2,1)}), bf16[4,224,256]{2,1,0:T(8,128)(2,1)S(1)}, u32[]{:S(2)}, u32[]{:S(2)}) async-start(bf16[4,224,256]{2,1,0:T(8,128)(2,1)} %get-tuple-element.9), calls=%async_computation.1 | async-start | bytes 917504 | tf_op jit(solution)/shard_map/all_to_all | solution.py:18
  91.2 7.9 %all-to-all-done.1.steps = bf16[4,224,256]{2,1,0:T(8,128)(2,1)S(1)} async-done(((bf16[4,224,256]{2,1,0:T(8,128)(2,1)}), bf16[4,224,256]{2,1,0:T(8,128)(2,1)S(1)}, u32[]{:S(2)}, u32[]{:S(2)}) %all-to-all-start.1) | async-done | bytes 458784 | tf_op jit(solution)/shard_map/all_to_all | solution.py:18
  99.1 0.9 copy-done.4
  100.1 0.9 copy-done.6
  101.0 3.3 %back.1 = (f32[224,2048]{1,0:T(8,128)}, f32[224,256]{1,0:T(8,128)}, f32[224,256]{1,0:T(8,128)}) custom-call(bf16[4,224,256]{2,1,0:T(8,128)(2,1)S(1)} %all-to-all-done.1.steps, f32[224,256]{1,0:T(8,128)S(1)} %copy-done.4, f32[224,256]{1,0:T(8,128)S(1)} %copy-done.6, bf16[128,2048]{1,0:T(8,128)(2,1)S(1)} %all_gather.3.rows.refs_0_, ...), custom_call_target="tpu_custom_call" | custom-call | tf_op jit(solution)/shard_map/back/pallas_call | solution.py:183
  (14 shorter events, 0.7 us)
Async XLA Ops:
  0.6 51.0 %collective-permute-start = (bf16[224,2048]{1,0:T(8,128)(2,1)}, bf16[224,2048]{1,0:T(8,128)(2,1)S(1)}, u32[]{:S(2)}, u32[]{:S(2)}) collective-permute-start(bf16[224,2048]{1,0:T(8,128)(2,1)} %own.5), channel_id=1, source_target_pairs={{0,4},{4,0},{1,5},{5,1},{2,6},{6,2},{3,7},{7,3},{8,12},{12,8},{9,1... | collective-permute-start | bytes 2752520 | tf_op jit(solution)/shard_map/ppermute | solution.py:163
  41.1 14.7 %collective-permute-start.3 = (bf16[128,2048]{1,0:T(8,128)(2,1)S(1)}, bf16[128,2048]{1,0:T(8,128)(2,1)S(1)}, u32[]{:S(2)}, u32[]{:S(2)}) collective-permute-start(bf16[128,2048]{1,0:T(8,128)(2,1)S(1)} %all_gather.3.rows.refs_0_), channel_id=1, source_target_pairs={{0,128},{128,256},{256,384},{384,0},{1,129},{129,257},{257,385},{3... | collective-permute-start | bytes 1572872 | tf_op jit(solution)/shard_map/ppermute | solution.py:148
  44.5 16.1 %collective-permute-start.2 = (bf16[128,2048]{1,0:T(8,128)(2,1)S(1)}, bf16[128,2048]{1,0:T(8,128)(2,1)S(1)}, u32[]{:S(2)}, u32[]{:S(2)}) collective-permute-start(bf16[128,2048]{1,0:T(8,128)(2,1)S(1)} %all_gather.3.rows.refs_0_), channel_id=1, source_target_pairs={{0,256},{128,384},{256,0},{384,128},{1,257},{129,385},{257,1},{385... | collective-permute-start | bytes 1572872 | tf_op jit(solution)/shard_map/ppermute | solution.py:148
  47.6 18.5 %collective-permute-start.1 = (bf16[128,2048]{1,0:T(8,128)(2,1)S(1)}, bf16[128,2048]{1,0:T(8,128)(2,1)S(1)}, u32[]{:S(2)}, u32[]{:S(2)}) collective-permute-start(bf16[128,2048]{1,0:T(8,128)(2,1)S(1)} %all_gather.3.rows.refs_0_), channel_id=1, source_target_pairs={{0,384},{128,0},{256,128},{384,256},{1,385},{129,1},{257,129},{385... | collective-permute-start | bytes 1572872 | tf_op jit(solution)/shard_map/ppermute | solution.py:148
  51.6 1.2 %copy-start = (bf16[224,2048]{1,0:T(8,128)(2,1)S(1)}, bf16[224,2048]{1,0:T(8,128)(2,1)}, u32[]{:S(2)}) copy-start(bf16[224,2048]{1,0:T(8,128)(2,1)} %own.5) | copy-start | bytes 2752516
  56.5 26.6 %copy-start.1 = (f32[224,256]{1,0:T(8,128)S(1)}, f32[224,256]{1,0:T(8,128)}, u32[]{:S(2)}) copy-start(f32[224,256]{1,0:T(8,128)} %first.1) | copy-start | bytes 688132
  56.5 26.6 %copy-start.2 = (f32[224,256]{1,0:T(8,128)S(1)}, f32[224,256]{1,0:T(8,128)}, u32[]{:S(2)}) copy-start(f32[224,256]{1,0:T(8,128)} %second.1) | copy-start | bytes 688132
  67.8 31.4 %collective-permute-start.5 = (bf16[256,2048]{1,0:T(8,128)(2,1)S(1)}, bf16[256,2048]{1,0:T(8,128)(2,1)}, u32[]{:S(2)}, u32[]{:S(2)}) collective-permute-start(bf16[256,2048]{1,0:T(8,128)(2,1)S(1)} %get-tuple-element.12.refs_2_), channel_id=1, source_target_pairs={{0,4},{4,0},{1,5},{5,1},{2,6},{6,2},{3,7},{7,3},{8,12},{12,8},{9,1... | collective-permute-start | bytes 3145736 | tf_op jit(solution)/shard_map/ppermute | solution.py:151
  69.7 13.4 %all-to-all-start = ((bf16[8,224,128]{2,1,0:T(8,128)(2,1)}), bf16[8,224,128]{2,1,0:T(8,128)(2,1)S(1)}, u32[]{:S(2)}, u32[]{:S(2)}) async-start(bf16[8,224,128]{2,1,0:T(8,128)(2,1)} %get-tuple-element.8), calls=%async_computation | async-start | bytes 917504 | tf_op jit(solution)/shard_map/all_to_all | solution.py:22
  74.9 16.3 %collective-permute-start.4 = (bf16[128,2048]{1,0:T(8,128)(2,1)S(1)}, bf16[128,2048]{1,0:T(8,128)(2,1)S(1)}, u32[]{:S(2)}, u32[]{:S(2)}) collective-permute-start(bf16[128,2048]{1,0:T(8,128)(2,1)S(1)} %all_gather.3.rows.refs_0_), channel_id=1, source_target_pairs={{0,4},{4,0},{1,5},{5,1},{2,6},{6,2},{3,7},{7,3},{8,12},{12,8},{9,1... | collective-permute-start | bytes 1572872 | tf_op jit(solution)/shard_map/ppermute | solution.py:151
  77.0 14.3 %collective-permute-start.6 = (bf16[128,2048]{1,0:T(8,128)(2,1)S(1)}, bf16[128,2048]{1,0:T(8,128)(2,1)}, u32[]{:S(2)}, u32[]{:S(2)}) collective-permute-start(bf16[128,2048]{1,0:T(8,128)(2,1)S(1)} %collective-permute-done.3.rows.refs_4_), channel_id=1, source_target_pairs={{0,4},{4,0},{1,5},{5,1},{2,6},{6,2},{3,7},{7,3},{8,12},{12,8},{9,1... | collective-permute-start | bytes 1572872 | tf_op jit(solution)/shard_map/ppermute | solution.py:151
  85.0 0.7 copy-start.3
  85.7 0.7 copy-start.5
  86.3 12.8 %all-to-all-start.1 = ((bf16[4,224,256]{2,1,0:T(8,128)(2,1)}), bf16[4,224,256]{2,1,0:T(8,128)(2,1)S(1)}, u32[]{:S(2)}, u32[]{:S(2)}) async-start(bf16[4,224,256]{2,1,0:T(8,128)(2,1)} %get-tuple-element.9), calls=%async_computation.1 | async-start | bytes 917504 | tf_op jit(solution)/shard_map/all_to_all | solution.py:18
  99.1 0.9 copy-start.4
  100.1 0.9 copy-start.6
